TPU v7x, 32 devices: a whole 2x2x4 slice. The times are simulated.
32 devices in a mesh: gx: 2 (over core), gy: 4 (over y, x), ma: 4 (over z).
Axes of the slice: x: 2, y: 2, z: 4, core: 2. Of those that a mesh axis runs over, the one named last changes fastest.
Arguments:
- object_field: float32 [2, 256, 1024], P(None, 'gx', 'gy'), may hold values from -5 to 5
- probe_modes: float32 [8, 2, 256, 256], P('ma'), may hold values from -1.5 to 1.5
- measured: float32 [2, 4, 2, 256, 256], P('gx', 'gy'), may hold values from 0.1 to 4
- positions: int32 [2, 4, 2, 2], P('gx', 'gy'), may hold values from 0 to 255, as said below
- slot_counts: int32 [2, 4], P('gx', 'gy'), may hold values from 1 to 2, as said below
Outputs:
- updated_object: float32 [2, 256, 1024], P(None, 'gx', 'gy')
Inputs may be any that keep to these rules, and one draw needn't show every extreme that they name: positions[a, b, s] holds a row 0 to 127 and a column 0 to 255 of tile (a, b); slots s >= slot_counts[a, b] are unused. `slot_counts`: some tile uses all 2 slots.
All inputs are finite; a program needn't handle non-finite values.
Results may differ from a plain program's by a relative error of at most 0.0023.
Values sent between devices are 32-bit elements; how exact they have to be, the bound alone decides.
A program may use at most 64 MiB of HBM per device.

v0:
```python
import math
import jax
import jax.numpy as jnp
import numpy as np
from jax import lax
from jax.sharding import PartitionSpec as P

OUTER = 2
DAMPING = 1.0


def dft_tables(patch_width):
    ladder = np.arange(patch_width)
    angles = ladder[:, None] * ladder[None, :] % patch_width * (2.0 * math.pi / patch_width)
    factor = 1.0 / math.sqrt(patch_width)
    real_part = np.cos(angles) * factor
    imag_part = -np.sin(angles) * factor
    table_one = np.block([[real_part, -imag_part], [imag_part, real_part]])
    table_two = np.block([[real_part, imag_part], [-imag_part, real_part]])
    return (jnp.asarray(table_one, jnp.bfloat16), jnp.asarray(table_two, jnp.bfloat16))


def shift_pair(low_part, high_part, axis):
    count = lax.axis_size(axis)
    forward = [(i, i + 1) for i in range(count - 1)]
    backward = [(target, source) for source, target in forward]
    return (lax.ppermute(high_part, axis, forward), lax.ppermute(low_part, axis, backward))


def widen(block, axis, dim, width):
    size = block.shape[dim]
    low, high = shift_pair(
        lax.slice_in_dim(block, 0, width, axis=dim),
        lax.slice_in_dim(block, size - width, None, axis=dim),
        axis,
    )
    return jnp.concatenate([low, block, high], axis=dim)


def fold(block, axis, dim, width):
    size = block.shape[dim]
    low, high = shift_pair(
        lax.slice_in_dim(block, 0, width, axis=dim),
        lax.slice_in_dim(block, size - width, None, axis=dim),
        axis,
    )
    middle = lax.slice_in_dim(block, width, size - width, axis=dim)
    pads = [(0, 0)] * 3
    pads[dim] = (0, size - 3 * width)
    first = jnp.pad(low, pads)
    pads[dim] = (size - 3 * width, 0)
    return middle + first + jnp.pad(high, pads)


def shards(object_field, probe_shard, measured, positions, slot_counts):
    patch = probe_shard.shape[-1]
    rim = patch // 2
    rows, cols = object_field.shape[1:]
    slots = measured.shape[2]
    share = patch // lax.axis_size("ma")
    first = lax.axis_index("ma") * share
    table_one, table_two = dft_tables(patch)
    left_one = lax.dynamic_slice_in_dim(table_one.reshape(2, patch, 2, patch), first, share, 1)
    right_two = table_two.reshape(2, patch, 2 * patch)
    left_two = lax.dynamic_slice_in_dim(table_two.reshape(2, patch, 2, patch), first, share, 3)
    targets = lax.dynamic_slice_in_dim(measured[0, 0], first, share, 1)
    centres = positions[0, 0]
    live = (jnp.arange(slots, dtype=jnp.int32) < slot_counts[0, 0]).astype(jnp.float32)
    live = live[:, None, None]
    anchor = jnp.zeros((), jnp.int32)
    probes = lax.all_gather(probe_shard, "ma", axis=0, tiled=True)
    modes = probes.shape[0]
    probe_real, probe_imag = (probes[None, :, 0], probes[None, :, 1])

    def spectra_of(tile):
        padded = widen(widen(tile, "gy", 2, rim), "gx", 1, rim)
        windows = jnp.stack(
            [
                lax.dynamic_slice(padded, (anchor, centres[s, 0], centres[s, 1]), (2, patch, patch))
                for s in range(slots)
            ]
        )
        real, imag = (windows[:, None, 0], windows[:, None, 1])
        waves = jnp.stack(
            [probe_real * real - probe_imag * imag, probe_real * imag + probe_imag * real], 2
        ).astype(jnp.bfloat16)
        halfway = jnp.einsum(
            "pqci,smcik->smpqk", left_one, waves, preferred_element_type=jnp.float32
        ).astype(jnp.bfloat16)
        return jnp.einsum("smcik,ckl->smil", halfway, right_two, preferred_element_type=jnp.float32)

    def mode_sum(first_spectra, second_spectra):
        product = first_spectra * second_spectra
        return jnp.sum(product[..., :patch] + product[..., patch:], axis=1)

    def project(weights, spectra):
        doubled = jnp.concatenate([weights, weights], -1)[:, None]
        scaled = (2.0 * spectra * doubled).astype(jnp.bfloat16)
        turned = jnp.einsum(
            "smik,kl->smil", scaled, table_one, preferred_element_type=jnp.float32
        ).astype(jnp.bfloat16)
        back = jnp.einsum(
            "pqci,smicl->smpql",
            left_two,
            turned.reshape(slots, modes, share, 2, patch),
            preferred_element_type=jnp.float32,
        )
        real = jnp.sum(probe_real * back[:, :, 0] + probe_imag * back[:, :, 1], axis=1)
        imag = jnp.sum(probe_real * back[:, :, 1] - probe_imag * back[:, :, 0], axis=1)
        pieces = jnp.stack([real, imag], 1)
        canvas = jnp.zeros((2, rows + patch, cols + patch), jnp.float32)
        room = jnp.pad(pieces, ((0, 0), (0, 0), (rows, rows), (cols, cols)))
        for s in range(slots):
            canvas = canvas + lax.dynamic_slice(
                room[s], (anchor, rows - centres[s, 0], cols - centres[s, 1]), canvas.shape
            )
        return lax.psum(fold(fold(canvas, "gx", 1, rim), "gy", 2, rim), "ma")

    current = object_field
    spectra = spectra_of(current)
    for outer_step in range(OUTER):
        misfit = live * (mode_sum(spectra, spectra) - targets)
        direction = -project(misfit, spectra)
        moved = spectra_of(direction)
        change = 2.0 * live * mode_sum(spectra, moved)
        sums = jnp.stack(
            [jnp.sum(direction * direction) / lax.axis_size("ma"), jnp.sum(change * change)]
        )
        sums = lax.psum(sums, ("gx", "gy", "ma"))
        step_size = sums[0] / (DAMPING * sums[0] + sums[1])
        current = current + step_size * direction
        if outer_step + 1 < OUTER:
            spectra = spectra + step_size * moved
    return current


def solution(mesh):
    return jax.shard_map(
        shards,
        mesh=mesh,
        in_specs=(
            P(None, "gx", "gy"),
            P("ma", None, None, None),
            P("gx", "gy", None, None, None),
            P("gx", "gy", None, None),
            P("gx", "gy"),
        ),
        out_specs=P(None, "gx", "gy"),
        check_vma=False,
    )
```

profile of v0, /device:TPU:0, one launch (start us, length us, event | category | flops | bytes accessed | tf_op | source)
XLA Modules:
  0.0 401.5 jit_solution(1194735594641044020)
XLA Ops:
  8.3 4.9 %collective-permute-start = (f32[2,128,128]{2,1,0:T(8,128)S(1)}, f32[2,128,128]{2,1,0:T(8,128)S(1)}, u32[]{:S(2)}, u32[]{:S(2)}) collective-permute-start(f32[2,128,128]{2,1,0:T(8,128)S(1)} %get-tuple-element.52), channel_id=1, source_target_pairs={{0,4},{4,8},{8,12},{1,5},{5,9},{9,13},{2,6},{6,10},{10,14},{3,7},{... | collective-permute-start | bytes 393224 | tf_op jit(solution)/shard_map/ppermute | solution.py:27
  16.9 3.8 collective-permute-done.1
  37.8 54.5 %all-gather.2.cloned.1.call-done = f32[8,2,256,256]{3,2,1,0:T(8,128)} async-done(((f32[2,2,256,256]{3,2,1,0:T(8,128)}), f32[8,2,256,256]{3,2,1,0:T(8,128)}) %all-gather.2.cloned.1.call-update) | async-done | bytes 4194320 | tf_op jit(solution)/shard_map/all_gather | solution.py:71
  92.4 4.0 slice_bitcast_fusion.5
  98.2 2.9 copy.45
  101.1 4.8 %subtract_convert_fusion.2 = (bf16[2,8,1,256,256]{4,3,2,1,0:T(8,128)(2,1)}, bf16[2,8,1,256,256]{4,3,2,1,0:T(8,128)(2,1)}) fusion(f32[2,256,256]{2,1,0:T(8,128)S(1)} %get-tuple-element.38, f32[8,256,256]{2,1,0:T(8,128)} %get-tuple-element.22, f32[2,256,256]{2,1,0:T(8,128)S(1)} %get-tuple-element.37, f32[8,256,256]{2,1,0:T(8,128)S(1)} %get-tuple-element.21), kind=kLoop, calls=%fused_computation.41 | loop fusion | flops 8388608 | bytes 9437184 | tf_op jit(solution)/shard_map/convert.4
  105.8 5.6 %bitcast_multiply_fusion.4 = (f32[2,8,64,512]{3,2,1,0:T(8,128)}, f32[2,8,64,512,1]{3,2,4,1,0:T(8,128)}) fusion(bf16[2,256,512,1,1]{2,1,0,4,3:T(8,128)(2,1)} %constant.64, bf16[2,8,1,256,256]{4,3,2,1,0:T(8,128)(2,1)} %get-tuple-element.20, bf16[2,8,1,256,256]{4,3,2,1,0:T(8,128)(2,1)} %get-tuple-element.19, bf16[2,256,2,256]{3,1,2,0:T(8,128)(2,1)} %constant.61, ...), kind=kOutput, calls=%fused_computation.53 | convolution fusion | flops 1083179008 | bytes 9043972 | tf_op jit(solution)/shard_map/smcik,ckl->smil/dot_general | solution.py:90
  129.6 3.4 collective-permute-start.6
  136.0 4.7 %collective-permute-done.7 = f32[2,128,128]{1,2,0:T(8,128)S(1)} collective-permute-done((f32[2,128,128]{1,2,0:T(8,128)S(1)}, f32[2,128,128]{1,2,0:T(8,128)S(1)}, u32[]{:S(2)}, u32[]{:S(2)}) %collective-permute-start.7) | collective-permute-done | bytes 131104 | tf_op jit(solution)/shard_map/ppermute | solution.py:27
  141.5 33.7 %all-reduce.9.cloned.1.call-done = f32[2,128,256]{1,2,0:T(8,128)} async-done(((f32[2,128,256]{1,2,0:T(8,128)}), f32[2,128,256]{1,2,0:T(8,128)}) %all-reduce.9.cloned.1.call-update) | async-done | bytes 262160 | tf_op jit(solution)/shard_map/psum | solution.py:117
  177.0 3.4 collective-permute-start.8
  182.9 4.4 %collective-permute-done.9 = f32[2,128,128]{1,2,0:T(8,128)S(1)} collective-permute-done((f32[2,128,128]{1,2,0:T(8,128)S(1)}, f32[2,128,128]{1,2,0:T(8,128)S(1)}, u32[]{:S(2)}, u32[]{:S(2)}) %collective-permute-start.9) | collective-permute-done | bytes 131104 | tf_op jit(solution)/shard_map/ppermute | solution.py:27
  197.8 3.4 subtract_convert_fusion.1
  201.1 6.2 %bitcast_multiply_fusion.2 = (f32[2,8,64,512]{3,2,1,0:T(8,128)}, f32[2,8,64,512,1]{3,2,4,1,0:T(8,128)}) fusion(f32[2,8,64,512,1]{3,2,4,1,0:T(8,128)} %get-tuple-element.62, bf16[2,256,512,1,1]{2,1,0,4,3:T(8,128)(2,1)S(1)} %copy-done.13, bf16[2,8,1,256,256]{4,3,2,1,0:T(8,128)(2,1)} %get-tuple-element.18, bf16[2,8,1,256,256]{4,3,2,1,0:T(8,128)(2,1)} %get-tuple-element.17, ...), kind=kOutput, calls=%fused_computation.49 | convolution fusion | flops 1083179008 | bytes 11141124 | tf_op jit(solution)/shard_map/smcik,ckl->smil/dot_general | solution.py:90
  210.4 39.8 %psum.29 = f32[2]{0:T(128)S(1)} all-reduce(f32[2]{0:T(128)S(1)} %pad_maximum_fusion.8), channel_id=1, replica_groups=mesh['gx'=2,'gy'=4,'ma'=4] {'gx','gy','ma'}, use_global_device_ids=true, to_apply=%region_7.8 | all-reduce | flops 2 | bytes 16 | tf_op jit(solution)/shard_map/psum | solution.py:129
  252.5 3.0 fusion.72
  269.8 4.2 %collective-permute-start.14 = (f32[2,128,128]{1,2,0:T(8,128)S(1)}, f32[2,128,128]{1,2,0:T(8,128)S(1)}, u32[]{:S(2)}, u32[]{:S(2)}) collective-permute-start(f32[2,128,128]{1,2,0:T(8,128)S(1)} %get-tuple-element.39), channel_id=1, source_target_pairs={{0,4},{4,8},{8,12},{1,5},{5,9},{9,13},{2,6},{6,10},{10,14},{3,7},{... | collective-permute-start | bytes 393224 | tf_op jit(solution)/shard_map/ppermute | solution.py:27
  277.0 4.7 %collective-permute-done.15 = f32[2,128,128]{1,2,0:T(8,128)S(1)} collective-permute-done((f32[2,128,128]{1,2,0:T(8,128)S(1)}, f32[2,128,128]{1,2,0:T(8,128)S(1)}, u32[]{:S(2)}, u32[]{:S(2)}) %collective-permute-start.15) | collective-permute-done | bytes 131104 | tf_op jit(solution)/shard_map/ppermute | solution.py:27
  282.5 34.8 %all-reduce.11.cloned.1.call-done = f32[2,128,256]{1,2,0:T(8,128)} async-done(((f32[2,128,256]{1,2,0:T(8,128)}), f32[2,128,256]{1,2,0:T(8,128)}) %all-reduce.11.cloned.1.call-update) | async-done | bytes 262160 | tf_op jit(solution)/shard_map/psum | solution.py:117
  318.9 3.4 collective-permute-start.16
  324.8 4.4 %collective-permute-done.17 = f32[2,128,128]{1,2,0:T(8,128)S(1)} collective-permute-done((f32[2,128,128]{1,2,0:T(8,128)S(1)}, f32[2,128,128]{1,2,0:T(8,128)S(1)}, u32[]{:S(2)}, u32[]{:S(2)}) %collective-permute-start.17) | collective-permute-done | bytes 131104 | tf_op jit(solution)/shard_map/ppermute | solution.py:27
  339.6 3.3 subtract_convert_fusion
  342.9 5.5 %bitcast_multiply_fusion = f32[2,8,64,512]{3,2,1,0:T(8,128)} fusion(f32[2,8,64,512]{3,2,1,0:T(8,128)} %copy-done.7, bf16[2,256,512,1,1]{2,1,0,4,3:T(8,128)(2,1)S(1)} %copy-done.14, bf16[2,8,1,256,256]{4,3,2,1,0:T(8,128)(2,1)} %get-tuple-element.16, bf16[2,8,1,256,256]{4,3,2,1,0:T(8,128)(2,1)} %get-tuple-element.15, bf16[2,256,2,256]{3,1,2,0:T(8,128)(2,1)} %constant.61, ...), kind=kOutput, calls=%fused_computation.46 | convolution fusion | flops 1083179008 | bytes 9043972 | tf_op jit(solution)/shard_map/smcik,ckl->smil/dot_general | solution.py:90
  351.8 39.8 %psum.31 = f32[2]{0:T(128)S(1)} all-reduce(f32[2]{0:T(128)S(1)} %pad_maximum_fusion.9), channel_id=1, replica_groups=mesh['gx'=2,'gy'=4,'ma'=4] {'gx','gy','ma'}, use_global_device_ids=true, to_apply=%region_15.16 | all-reduce | flops 2 | bytes 16 | tf_op jit(solution)/shard_map/psum | solution.py:129
  (137 shorter events, 87.2 us)
Async XLA Ops:
  6.5 85.9 %all-gather.2.cloned.1.call-start = ((), (), s32[]{:S(2)}) async-start(), calls=%async_computation | async-start | bytes 5242880 | tf_op jit(solution)/shard_map/all_gather | solution.py:71
  7.3 168.0 %all-reduce.9.cloned.1.call-start = ((), (), s32[]{:S(2)}) async-start(), calls=%async_computation.1 | async-start | bytes 524288 | tf_op jit(solution)/shard_map/psum | solution.py:117
  8.3 7.6 %collective-permute-start = (f32[2,128,128]{2,1,0:T(8,128)S(1)}, f32[2,128,128]{2,1,0:T(8,128)S(1)}, u32[]{:S(2)}, u32[]{:S(2)}) collective-permute-start(f32[2,128,128]{2,1,0:T(8,128)S(1)} %get-tuple-element.52), channel_id=1, source_target_pairs={{0,4},{4,8},{8,12},{1,5},{5,9},{9,13},{2,6},{6,10},{10,14},{3,7},{... | collective-permute-start | bytes 393224 | tf_op jit(solution)/shard_map/ppermute | solution.py:27
  13.2 7.5 %collective-permute-start.1 = (f32[2,128,128]{2,1,0:T(8,128)S(1)}, f32[2,128,128]{2,1,0:T(8,128)S(1)}, u32[]{:S(2)}, u32[]{:S(2)}) collective-permute-start(f32[2,128,128]{2,1,0:T(8,128)S(1)} %get-tuple-element.51), channel_id=1, source_target_pairs={{4,0},{8,4},{12,8},{5,1},{9,5},{13,9},{6,2},{10,6},{14,10},{7,3},{... | collective-permute-start | bytes 393224 | tf_op jit(solution)/shard_map/ppermute | solution.py:27
  20.7 16.6 %collective-permute-start.2 = (f32[2,128,512]{2,1,0:T(8,128)S(1)}, f32[2,128,512]{2,1,0:T(8,128)S(1)}, u32[]{:S(2)}, u32[]{:S(2)}) collective-permute-start(f32[2,128,512]{2,1,0:T(8,128)S(1)} %constant_dynamic-update-slice_fusion), channel_id=1, source_target_pairs={{0,16},{1,17},{2,18},{3,19},{4,20},{5,21},{6,22},{7,23},{8,24},{9,... | collective-permute-start | bytes 1572872 | tf_op jit(solution)/shard_map/ppermute | solution.py:27
  22.0 15.2 %collective-permute-start.3 = (f32[2,128,512]{2,1,0:T(8,128)S(1)}, f32[2,128,512]{2,1,0:T(8,128)S(1)}, u32[]{:S(2)}, u32[]{:S(2)}) collective-permute-start(f32[2,128,512]{2,1,0:T(8,128)S(1)} %constant_dynamic-update-slice_fusion), channel_id=1, source_target_pairs={{16,0},{17,1},{18,2},{19,3},{20,4},{21,5},{22,6},{23,7},{24,8},{25... | collective-permute-start | bytes 1572872 | tf_op jit(solution)/shard_map/ppermute | solution.py:27
  124.0 3.1 collective-permute-start.4
  125.6 3.8 collective-permute-start.5
  129.6 6.4 %collective-permute-start.6 = (f32[2,128,128]{1,2,0:T(8,128)S(1)}, f32[2,128,128]{1,2,0:T(8,128)S(1)}, u32[]{:S(2)}, u32[]{:S(2)}) collective-permute-start(f32[2,128,128]{1,2,0:T(8,128)S(1)} %get-tuple-element.41), channel_id=1, source_target_pairs={{0,4},{4,8},{8,12},{1,5},{5,9},{9,13},{2,6},{6,10},{10,14},{3,7},{... | collective-permute-start | bytes 393224 | tf_op jit(solution)/shard_map/ppermute | solution.py:27
  132.9 7.8 %collective-permute-start.7 = (f32[2,128,128]{1,2,0:T(8,128)S(1)}, f32[2,128,128]{1,2,0:T(8,128)S(1)}, u32[]{:S(2)}, u32[]{:S(2)}) collective-permute-start(f32[2,128,128]{1,2,0:T(8,128)S(1)} %get-tuple-element.42), channel_id=1, source_target_pairs={{4,0},{8,4},{12,8},{5,1},{9,5},{13,9},{6,2},{10,6},{14,10},{7,3},{... | collective-permute-start | bytes 393224 | tf_op jit(solution)/shard_map/ppermute | solution.py:27
  141.5 175.8 %all-reduce.11.cloned.1.call-start = ((), (), s32[]{:S(2)}) async-start(), calls=%async_computation.2 | async-start | bytes 524288 | tf_op jit(solution)/shard_map/psum | solution.py:117
  177.0 5.9 %collective-permute-start.8 = (f32[2,128,128]{1,2,0:T(8,128)S(1)}, f32[2,128,128]{1,2,0:T(8,128)S(1)}, u32[]{:S(2)}, u32[]{:S(2)}) collective-permute-start(f32[2,128,128]{1,2,0:T(8,128)S(1)} %get-tuple-element.49), channel_id=1, source_target_pairs={{0,4},{4,8},{8,12},{1,5},{5,9},{9,13},{2,6},{6,10},{10,14},{3,7},{... | collective-permute-start | bytes 393224 | tf_op jit(solution)/shard_map/ppermute | solution.py:27
  180.4 6.9 %collective-permute-start.9 = (f32[2,128,128]{1,2,0:T(8,128)S(1)}, f32[2,128,128]{1,2,0:T(8,128)S(1)}, u32[]{:S(2)}, u32[]{:S(2)}) collective-permute-start(f32[2,128,128]{1,2,0:T(8,128)S(1)} %get-tuple-element.50), channel_id=1, source_target_pairs={{4,0},{8,4},{12,8},{5,1},{9,5},{13,9},{6,2},{10,6},{14,10},{7,3},{... | collective-permute-start | bytes 393224 | tf_op jit(solution)/shard_map/ppermute | solution.py:27
  187.9 3.5 collective-permute-start.10
  189.3 3.9 collective-permute-start.11
  264.5 2.8 collective-permute-start.12
  265.8 3.8 collective-permute-start.13
  269.8 7.2 %collective-permute-start.14 = (f32[2,128,128]{1,2,0:T(8,128)S(1)}, f32[2,128,128]{1,2,0:T(8,128)S(1)}, u32[]{:S(2)}, u32[]{:S(2)}) collective-permute-start(f32[2,128,128]{1,2,0:T(8,128)S(1)} %get-tuple-element.39), channel_id=1, source_target_pairs={{0,4},{4,8},{8,12},{1,5},{5,9},{9,13},{2,6},{6,10},{10,14},{3,7},{... | collective-permute-start | bytes 393224 | tf_op jit(solution)/shard_map/ppermute | solution.py:27
  274.0 7.8 %collective-permute-start.15 = (f32[2,128,128]{1,2,0:T(8,128)S(1)}, f32[2,128,128]{1,2,0:T(8,128)S(1)}, u32[]{:S(2)}, u32[]{:S(2)}) collective-permute-start(f32[2,128,128]{1,2,0:T(8,128)S(1)} %get-tuple-element.40), channel_id=1, source_target_pairs={{4,0},{8,4},{12,8},{5,1},{9,5},{13,9},{6,2},{10,6},{14,10},{7,3},{... | collective-permute-start | bytes 393224 | tf_op jit(solution)/shard_map/ppermute | solution.py:27
  318.9 5.9 %collective-permute-start.16 = (f32[2,128,128]{1,2,0:T(8,128)S(1)}, f32[2,128,128]{1,2,0:T(8,128)S(1)}, u32[]{:S(2)}, u32[]{:S(2)}) collective-permute-start(f32[2,128,128]{1,2,0:T(8,128)S(1)} %get-tuple-element.45), channel_id=1, source_target_pairs={{0,4},{4,8},{8,12},{1,5},{5,9},{9,13},{2,6},{6,10},{10,14},{3,7},{... | collective-permute-start | bytes 393224 | tf_op jit(solution)/shard_map/ppermute | solution.py:27
  322.3 6.9 %collective-permute-start.17 = (f32[2,128,128]{1,2,0:T(8,128)S(1)}, f32[2,128,128]{1,2,0:T(8,128)S(1)}, u32[]{:S(2)}, u32[]{:S(2)}) collective-permute-start(f32[2,128,128]{1,2,0:T(8,128)S(1)} %get-tuple-element.46), channel_id=1, source_target_pairs={{4,0},{8,4},{12,8},{5,1},{9,5},{13,9},{6,2},{10,6},{14,10},{7,3},{... | collective-permute-start | bytes 393224 | tf_op jit(solution)/shard_map/ppermute | solution.py:27
  329.9 3.4 collective-permute-start.18
  331.2 3.9 collective-permute-start.19
  348.4 45.6 %copy-start.12 = (f32[2,128,256]{1,2,0:T(8,128)S(1)}, f32[2,128,256]{1,2,0:T(8,128)}, u32[]{:S(2)}) copy-start(f32[2,128,256]{1,2,0:T(8,128)} %all-reduce.11.cloned.1.call-done) | copy-start | bytes 786436
  (17 other events, 96.5 us)
Sparse Core Ops, SparseCore 0:
  8.9 83.4 all-gather.1
  141.6 33.6 all-reduce.8
  282.6 34.6 all-reduce.10
where the time goes:
time: 403 us; the launch traced here: 402 us
  waiting for transfers between devices  162 us (40%)
  blocking collectives  79.6 us (20%)
  other arithmetic  42 us (10%)
  starting transfers between devices  39.5 us (10%)
  between operations  31.9 us (8%)
  matrix products  24.5 us (6%)
  local copies, waits for them, and re-layouts  22.3 us (6%)
    psum x2, blocking collectives, shards(): sums = lax.psum(sums, ('gx', 'gy', 'ma'))  79.6 us
    psum x2, waiting for transfers between devices, project(): return lax.psum(fold(fold(canvas, 'gx', 1, rim), 'gy', 2, rim), 'ma')  68.5 us
    all_gather x1, waiting for transfers between devices, shards(): probes = lax.all_gather(probe_shard, 'ma', axis=0, tiled=True)  54.5 us
    ppermute x10, waiting for transfers between devices, shift_pair(): lax.ppermute(low_part, axis, backward)  30.2 us
    ppermute x10, starting transfers between devices, shift_pair(): lax.ppermute(high_part, axis, forward)  26.1 us
    dot_general x3, matrix products, spectra_of(): jnp.einsum('smcik,ckl->smil', halfway, right_two, preferred_element_type=...  17.3 us
    ppermute x10, starting transfers between devices, shift_pair(): lax.ppermute(low_part, axis, backward)  13.3 us
    another operation x3, other arithmetic  11.4 us
  transfers between devices with their start and end apart: 23, of which 19 were waited for; matrix products, arithmetic and copies ran while one was open for 1% of the time, Pallas kernels for 0%

commit v1 on v0

--- a/solution.py
+++ b/solution.py
@@ -114,7 +114,7 @@
             canvas = canvas + lax.dynamic_slice(
                 room[s], (anchor, rows - centres[s, 0], cols - centres[s, 1]), canvas.shape
             )
-        return lax.psum(fold(fold(canvas, "gx", 1, rim), "gy", 2, rim), "ma")
+        return jnp.sum(lax.all_gather(fold(fold(canvas, "gx", 1, rim), "gy", 2, rim), "ma"), axis=0)
 
     current = object_field
     spectra = spectra_of(current)

time: 403 us -> 386 us (0.958)
  waiting for transfers between devices: 162 us -> 142 us
  starting transfers between devices: 39.5 us -> 47.5 us
    psum x2 -> x0, waiting for transfers between devices: 68.5 us -> none  [project(): return lax.psum(fold(fold(canvas, 'gx', 1, rim), 'gy', 2, rim), 'ma')]
    all_gather x0 -> x2, waiting for transfers between devices: none -> 53 us  [project(): lax.all_gather(fold(fold(canvas, 'gx', 1, rim), 'gy', 2, rim), 'ma')]
    ppermute x10, starting transfers between devices: 26.1 us -> 34.6 us  [shift_pair(): lax.ppermute(high_part, axis, forward)]
where the time goes in v1:
time: 386 us; the launch traced here: 384 us
  waiting for transfers between devices  142 us (37%)
  blocking collectives  78.9 us (20%)
  starting transfers between devices  47.5 us (12%)
  other arithmetic  39.4 us (10%)
  between operations  32.3 us (8%)
  matrix products  23.1 us (6%)
  local copies, waits for them, and re-layouts  21.2 us (5%)
    psum x2, blocking collectives, shards(): sums = lax.psum(sums, ('gx', 'gy', 'ma'))  78.9 us
    all_gather x2, waiting for transfers between devices, project(): lax.all_gather(fold(fold(canvas, 'gx', 1, rim), 'gy', 2, rim), 'ma')  53 us
    all_gather x1, waiting for transfers between devices, shards(): probes = lax.all_gather(probe_shard, 'ma', axis=0, tiled=True)  52.5 us
    ppermute x10, starting transfers between devices, shift_pair(): lax.ppermute(high_part, axis, forward)  34.6 us
    ppermute x10, waiting for transfers between devices, shift_pair(): lax.ppermute(low_part, axis, backward)  27.2 us
    dot_general x3, matrix products, spectra_of(): jnp.einsum('smcik,ckl->smil', halfway, right_two, preferred_element_type=...  16 us
    ppermute x10, starting transfers between devices, shift_pair(): lax.ppermute(low_part, axis, backward)  12.9 us
    another operation x3, other arithmetic  11.5 us
  transfers between devices with their start and end apart: 23, of which 19 were waited for; matrix products, arithmetic and copies ran while one was open for 1% of the time, Pallas kernels for 0%

profile of v1, /device:TPU:0, one launch (start us, length us, event | category | flops | bytes accessed | tf_op | source)
XLA Modules:
  0.0 384.3 jit_solution(9204904624788202651)
XLA Ops:
  8.3 4.9 %collective-permute-start = (f32[2,128,128]{2,1,0:T(8,128)S(1)}, f32[2,128,128]{2,1,0:T(8,128)S(1)}, u32[]{:S(2)}, u32[]{:S(2)}) collective-permute-start(f32[2,128,128]{2,1,0:T(8,128)S(1)} %get-tuple-element.52), channel_id=1, source_target_pairs={{0,4},{4,8},{8,12},{1,5},{5,9},{9,13},{2,6},{6,10},{10,14},{3,7},{... | collective-permute-start | bytes 393224 | tf_op jit(solution)/shard_map/ppermute | solution.py:27
  16.9 3.8 collective-permute-done.1
  39.9 52.5 %all-gather.6.cloned.1.call-done = f32[8,2,256,256]{3,2,1,0:T(8,128)} async-done(((f32[2,2,256,256]{3,2,1,0:T(8,128)}), f32[8,2,256,256]{3,2,1,0:T(8,128)}) %all-gather.6.cloned.1.call-update) | async-done | bytes 4194320 | tf_op jit(solution)/shard_map/all_gather | solution.py:71
  92.4 4.0 %slice_bitcast_fusion.5 = (f32[8,256,256]{2,1,0:T(8,128)S(1)}, f32[8,256,256]{2,1,0:T(8,128)}) fusion(f32[8,2,256,256]{3,2,1,0:T(8,128)} %all-gather.6.cloned.1.call-done), kind=kLoop, calls=%fused_computation.38 | loop fusion | bytes 8388608 | tf_op jit(solution)/shard_map/mul | solution.py:108
  101.1 4.8 %subtract_convert_fusion.2 = (bf16[2,8,1,256,256]{4,3,2,1,0:T(8,128)(2,1)}, bf16[2,8,1,256,256]{4,3,2,1,0:T(8,128)(2,1)}) fusion(f32[2,256,256]{2,1,0:T(8,128)S(1)} %get-tuple-element.38, f32[8,256,256]{2,1,0:T(8,128)} %get-tuple-element.22, f32[2,256,256]{2,1,0:T(8,128)S(1)} %get-tuple-element.37, f32[8,256,256]{2,1,0:T(8,128)S(1)} %get-tuple-element.21), kind=kLoop, calls=%fused_computation.34 | loop fusion | flops 8388608 | bytes 9437184 | tf_op jit(solution)/shard_map/convert.4
  105.8 5.6 %bitcast_multiply_fusion.4 = (f32[2,8,64,512]{3,2,1,0:T(8,128)}, f32[2,8,64,512,1]{3,2,4,1,0:T(8,128)}) fusion(bf16[2,256,512,1,1]{2,1,0,4,3:T(8,128)(2,1)} %constant.64, bf16[2,8,1,256,256]{4,3,2,1,0:T(8,128)(2,1)} %get-tuple-element.20, bf16[2,8,1,256,256]{4,3,2,1,0:T(8,128)(2,1)} %get-tuple-element.19, bf16[2,256,2,256]{3,1,2,0:T(8,128)(2,1)} %constant.61, ...), kind=kOutput, calls=%fused_computation.46 | convolution fusion | flops 1083179008 | bytes 9043972 | tf_op jit(solution)/shard_map/smcik,ckl->smil/dot_general | solution.py:90
  129.5 3.4 collective-permute-start.6
  135.9 4.7 %collective-permute-done.7 = f32[2,128,128]{1,2,0:T(8,128)S(1)} collective-permute-done((f32[2,128,128]{1,2,0:T(8,128)S(1)}, f32[2,128,128]{1,2,0:T(8,128)S(1)}, u32[]{:S(2)}, u32[]{:S(2)}) %collective-permute-start.7) | collective-permute-done | bytes 131104 | tf_op jit(solution)/shard_map/ppermute | solution.py:27
  141.6 26.1 %all-gather.8.cloned.1.call-done = f32[8,128,256]{2,1,0:T(8,128)} async-done(((f32[2,128,256]{2,1,0:T(8,128)}), f32[8,128,256]{2,1,0:T(8,128)}) %all-gather.8.cloned.1.call-update) | async-done | bytes 1048592 | tf_op jit(solution)/shard_map/all_gather | solution.py:117
  169.8 3.4 collective-permute-start.8
  175.7 4.7 %collective-permute-done.9 = f32[2,128,128]{2,1,0:T(8,128)S(1)} collective-permute-done((f32[2,128,128]{2,1,0:T(8,128)S(1)}, f32[2,128,128]{2,1,0:T(8,128)S(1)}, u32[]{:S(2)}, u32[]{:S(2)}) %collective-permute-start.9) | collective-permute-done | bytes 131104 | tf_op jit(solution)/shard_map/ppermute | solution.py:27
  181.7 4.7 %collective-permute-start.10 = (f32[2,128,512]{2,1,0:T(8,128)S(1)}, f32[2,128,512]{2,1,0:T(8,128)}, u32[]{:S(2)}, u32[]{:S(2)}) collective-permute-start(f32[2,128,512]{2,1,0:T(8,128)S(1)} %pad_maximum_fusion.6), channel_id=1, source_target_pairs={{0,16},{1,17},{2,18},{3,19},{4,20},{5,21},{6,22},{7,23},{8,24},{9,... | collective-permute-start | bytes 1572872 | tf_op jit(solution)/shard_map/ppermute | solution.py:27
  190.2 3.4 subtract_convert_fusion.1
  193.6 6.2 %bitcast_multiply_fusion.2 = (f32[2,8,64,512]{3,2,1,0:T(8,128)}, f32[2,8,64,512,1]{3,2,4,1,0:T(8,128)}) fusion(f32[2,8,64,512,1]{3,2,4,1,0:T(8,128)} %get-tuple-element.62, bf16[2,256,512,1,1]{2,1,0,4,3:T(8,128)(2,1)S(1)} %copy-done.11, bf16[2,8,1,256,256]{4,3,2,1,0:T(8,128)(2,1)} %get-tuple-element.18, bf16[2,8,1,256,256]{4,3,2,1,0:T(8,128)(2,1)} %get-tuple-element.17, ...), kind=kOutput, calls=%fused_computation.42 | convolution fusion | flops 1083179008 | bytes 11141124 | tf_op jit(solution)/shard_map/smcik,ckl->smil/dot_general | solution.py:90
  202.9 39.5 %psum.14 = f32[2]{0:T(128)S(1)} all-reduce(f32[2]{0:T(128)S(1)} %pad_maximum_fusion.8), channel_id=1, replica_groups=mesh['gx'=2,'gy'=4,'ma'=4] {'gx','gy','ma'}, use_global_device_ids=true, to_apply=%region_7.8 | all-reduce | flops 2 | bytes 16 | tf_op jit(solution)/shard_map/psum | solution.py:129
  262.1 4.2 %collective-permute-start.14 = (f32[2,128,128]{1,2,0:T(8,128)S(1)}, f32[2,128,128]{1,2,0:T(8,128)S(1)}, u32[]{:S(2)}, u32[]{:S(2)}) collective-permute-start(f32[2,128,128]{1,2,0:T(8,128)S(1)} %get-tuple-element.39), channel_id=1, source_target_pairs={{0,4},{4,8},{8,12},{1,5},{5,9},{9,13},{2,6},{6,10},{10,14},{3,7},{... | collective-permute-start | bytes 393224 | tf_op jit(solution)/shard_map/ppermute | solution.py:27
  269.4 4.7 %collective-permute-done.15 = f32[2,128,128]{1,2,0:T(8,128)S(1)} collective-permute-done((f32[2,128,128]{1,2,0:T(8,128)S(1)}, f32[2,128,128]{1,2,0:T(8,128)S(1)}, u32[]{:S(2)}, u32[]{:S(2)}) %collective-permute-start.15) | collective-permute-done | bytes 131104 | tf_op jit(solution)/shard_map/ppermute | solution.py:27
  275.0 26.9 %all-gather.10.cloned.1.call-done = f32[8,128,256]{2,1,0:T(8,128)} async-done(((f32[2,128,256]{2,1,0:T(8,128)}), f32[8,128,256]{2,1,0:T(8,128)}) %all-gather.10.cloned.1.call-update) | async-done | bytes 1048592 | tf_op jit(solution)/shard_map/all_gather | solution.py:117
  304.0 3.4 collective-permute-start.16
  309.9 4.7 %collective-permute-done.17 = f32[2,128,128]{2,1,0:T(8,128)S(1)} collective-permute-done((f32[2,128,128]{2,1,0:T(8,128)S(1)}, f32[2,128,128]{2,1,0:T(8,128)S(1)}, u32[]{:S(2)}, u32[]{:S(2)}) %collective-permute-start.17) | collective-permute-done | bytes 131104 | tf_op jit(solution)/shard_map/ppermute | solution.py:27
  317.4 4.6 %collective-permute-start.18 = (f32[2,128,512]{2,1,0:T(8,128)}, f32[2,128,512]{2,1,0:T(8,128)}, u32[]{:S(2)}, u32[]{:S(2)}) collective-permute-start(f32[2,128,512]{2,1,0:T(8,128)} %pad_maximum_fusion.7), channel_id=1, source_target_pairs={{0,16},{1,17},{2,18},{3,19},{4,20},{5,21},{6,22},{7,23},{8,24},{9,... | collective-permute-start | bytes 1572872 | tf_op jit(solution)/shard_map/ppermute | solution.py:27
  326.0 3.3 subtract_convert_fusion
  329.3 4.2 %bitcast_multiply_fusion = f32[2,8,64,512]{3,2,1,0:T(8,128)S(1)} fusion(f32[2,8,64,512]{3,2,1,0:T(8,128)} %copy-done.7, bf16[2,256,512,1,1]{2,1,0,4,3:T(8,128)(2,1)S(1)} %copy-done.11, bf16[2,8,1,256,256]{4,3,2,1,0:T(8,128)(2,1)} %get-tuple-element.16, bf16[2,8,1,256,256]{4,3,2,1,0:T(8,128)(2,1)} %get-tuple-element.15, ...), kind=kOutput, calls=%fused_computation.39 | convolution fusion | flops 1083179008 | bytes 9043972 | tf_op jit(solution)/shard_map/smcik,ckl->smil/dot_general | solution.py:90
  335.1 39.5 %psum.15 = f32[2]{0:T(128)S(1)} all-reduce(f32[2]{0:T(128)S(1)} %pad_maximum_fusion.9), channel_id=1, replica_groups=mesh['gx'=2,'gy'=4,'ma'=4] {'gx','gy','ma'}, use_global_device_ids=true, to_apply=%region_15.16 | all-reduce | flops 2 | bytes 16 | tf_op jit(solution)/shard_map/psum | solution.py:129
  (127 shorter events, 85.0 us)
Async XLA Ops:
  6.5 85.9 %all-gather.6.cloned.1.call-start = ((), (), s32[]{:S(2)}) async-start(), calls=%async_computation | async-start | bytes 5242880 | tf_op jit(solution)/shard_map/all_gather | solution.py:71
  7.3 160.5 %all-gather.8.cloned.1.call-start = ((), (), s32[]{:S(2)}) async-start(), calls=%async_computation.1 | async-start | bytes 1310720 | tf_op jit(solution)/shard_map/all_gather | solution.py:117
  8.3 7.6 %collective-permute-start = (f32[2,128,128]{2,1,0:T(8,128)S(1)}, f32[2,128,128]{2,1,0:T(8,128)S(1)}, u32[]{:S(2)}, u32[]{:S(2)}) collective-permute-start(f32[2,128,128]{2,1,0:T(8,128)S(1)} %get-tuple-element.52), channel_id=1, source_target_pairs={{0,4},{4,8},{8,12},{1,5},{5,9},{9,13},{2,6},{6,10},{10,14},{3,7},{... | collective-permute-start | bytes 393224 | tf_op jit(solution)/shard_map/ppermute | solution.py:27
  13.2 7.5 %collective-permute-start.1 = (f32[2,128,128]{2,1,0:T(8,128)S(1)}, f32[2,128,128]{2,1,0:T(8,128)S(1)}, u32[]{:S(2)}, u32[]{:S(2)}) collective-permute-start(f32[2,128,128]{2,1,0:T(8,128)S(1)} %get-tuple-element.51), channel_id=1, source_target_pairs={{4,0},{8,4},{12,8},{5,1},{9,5},{13,9},{6,2},{10,6},{14,10},{7,3},{... | collective-permute-start | bytes 393224 | tf_op jit(solution)/shard_map/ppermute | solution.py:27
  20.7 18.6 %collective-permute-start.3 = (f32[2,128,512]{2,1,0:T(8,128)S(1)}, f32[2,128,512]{2,1,0:T(8,128)S(1)}, u32[]{:S(2)}, u32[]{:S(2)}) collective-permute-start(f32[2,128,512]{2,1,0:T(8,128)S(1)} %constant_dynamic-update-slice_fusion), channel_id=1, source_target_pairs={{16,0},{17,1},{18,2},{19,3},{20,4},{21,5},{22,6},{23,7},{24,8},{25... | collective-permute-start | bytes 1572872 | tf_op jit(solution)/shard_map/ppermute | solution.py:27
  22.0 17.3 %collective-permute-start.2 = (f32[2,128,512]{2,1,0:T(8,128)S(1)}, f32[2,128,512]{2,1,0:T(8,128)S(1)}, u32[]{:S(2)}, u32[]{:S(2)}) collective-permute-start(f32[2,128,512]{2,1,0:T(8,128)S(1)} %constant_dynamic-update-slice_fusion), channel_id=1, source_target_pairs={{0,16},{1,17},{2,18},{3,19},{4,20},{5,21},{6,22},{7,23},{8,24},{9,... | collective-permute-start | bytes 1572872 | tf_op jit(solution)/shard_map/ppermute | solution.py:27
  123.9 3.1 collective-permute-start.4
  125.6 3.8 collective-permute-start.5
  129.5 6.4 %collective-permute-start.6 = (f32[2,128,128]{1,2,0:T(8,128)S(1)}, f32[2,128,128]{1,2,0:T(8,128)S(1)}, u32[]{:S(2)}, u32[]{:S(2)}) collective-permute-start(f32[2,128,128]{1,2,0:T(8,128)S(1)} %get-tuple-element.41), channel_id=1, source_target_pairs={{0,4},{4,8},{8,12},{1,5},{5,9},{9,13},{2,6},{6,10},{10,14},{3,7},{... | collective-permute-start | bytes 393224 | tf_op jit(solution)/shard_map/ppermute | solution.py:27
  132.9 7.8 %collective-permute-start.7 = (f32[2,128,128]{1,2,0:T(8,128)S(1)}, f32[2,128,128]{1,2,0:T(8,128)S(1)}, u32[]{:S(2)}, u32[]{:S(2)}) collective-permute-start(f32[2,128,128]{1,2,0:T(8,128)S(1)} %get-tuple-element.42), channel_id=1, source_target_pairs={{4,0},{8,4},{12,8},{5,1},{9,5},{13,9},{6,2},{10,6},{14,10},{7,3},{... | collective-permute-start | bytes 393224 | tf_op jit(solution)/shard_map/ppermute | solution.py:27
  141.6 160.3 %all-gather.10.cloned.1.call-start = ((), (), s32[]{:S(2)}) async-start(), calls=%async_computation.2 | async-start | bytes 1310720 | tf_op jit(solution)/shard_map/all_gather | solution.py:117
  169.8 5.9 %collective-permute-start.8 = (f32[2,128,128]{2,1,0:T(8,128)S(1)}, f32[2,128,128]{2,1,0:T(8,128)S(1)}, u32[]{:S(2)}, u32[]{:S(2)}) collective-permute-start(f32[2,128,128]{2,1,0:T(8,128)S(1)} %get-tuple-element.49), channel_id=1, source_target_pairs={{0,4},{4,8},{8,12},{1,5},{5,9},{9,13},{2,6},{6,10},{10,14},{3,7},{... | collective-permute-start | bytes 393224 | tf_op jit(solution)/shard_map/ppermute | solution.py:27
  173.2 7.2 %collective-permute-start.9 = (f32[2,128,128]{2,1,0:T(8,128)S(1)}, f32[2,128,128]{2,1,0:T(8,128)S(1)}, u32[]{:S(2)}, u32[]{:S(2)}) collective-permute-start(f32[2,128,128]{2,1,0:T(8,128)S(1)} %get-tuple-element.50), channel_id=1, source_target_pairs={{4,0},{8,4},{12,8},{5,1},{9,5},{13,9},{6,2},{10,6},{14,10},{7,3},{... | collective-permute-start | bytes 393224 | tf_op jit(solution)/shard_map/ppermute | solution.py:27
  180.4 6.6 %collective-permute-start.11 = (f32[2,128,512]{2,1,0:T(8,128)S(1)}, f32[2,128,512]{2,1,0:T(8,128)}, u32[]{:S(2)}, u32[]{:S(2)}) collective-permute-start(f32[2,128,512]{2,1,0:T(8,128)S(1)} %pad_maximum_fusion.6), channel_id=1, source_target_pairs={{16,0},{17,1},{18,2},{19,3},{20,4},{21,5},{22,6},{23,7},{24,8},{25... | collective-permute-start | bytes 1572872 | tf_op jit(solution)/shard_map/ppermute | solution.py:27
  181.7 5.5 %collective-permute-start.10 = (f32[2,128,512]{2,1,0:T(8,128)S(1)}, f32[2,128,512]{2,1,0:T(8,128)}, u32[]{:S(2)}, u32[]{:S(2)}) collective-permute-start(f32[2,128,512]{2,1,0:T(8,128)S(1)} %pad_maximum_fusion.6), channel_id=1, source_target_pairs={{0,16},{1,17},{2,18},{3,19},{4,20},{5,21},{6,22},{7,23},{8,24},{9,... | collective-permute-start | bytes 1572872 | tf_op jit(solution)/shard_map/ppermute | solution.py:27
  256.9 2.8 collective-permute-start.12
  258.2 3.8 collective-permute-start.13
  262.1 7.2 %collective-permute-start.14 = (f32[2,128,128]{1,2,0:T(8,128)S(1)}, f32[2,128,128]{1,2,0:T(8,128)S(1)}, u32[]{:S(2)}, u32[]{:S(2)}) collective-permute-start(f32[2,128,128]{1,2,0:T(8,128)S(1)} %get-tuple-element.39), channel_id=1, source_target_pairs={{0,4},{4,8},{8,12},{1,5},{5,9},{9,13},{2,6},{6,10},{10,14},{3,7},{... | collective-permute-start | bytes 393224 | tf_op jit(solution)/shard_map/ppermute | solution.py:27
  266.3 7.7 %collective-permute-start.15 = (f32[2,128,128]{1,2,0:T(8,128)S(1)}, f32[2,128,128]{1,2,0:T(8,128)S(1)}, u32[]{:S(2)}, u32[]{:S(2)}) collective-permute-start(f32[2,128,128]{1,2,0:T(8,128)S(1)} %get-tuple-element.40), channel_id=1, source_target_pairs={{4,0},{8,4},{12,8},{5,1},{9,5},{13,9},{6,2},{10,6},{14,10},{7,3},{... | collective-permute-start | bytes 393224 | tf_op jit(solution)/shard_map/ppermute | solution.py:27
  304.0 5.9 %collective-permute-start.16 = (f32[2,128,128]{2,1,0:T(8,128)S(1)}, f32[2,128,128]{2,1,0:T(8,128)S(1)}, u32[]{:S(2)}, u32[]{:S(2)}) collective-permute-start(f32[2,128,128]{2,1,0:T(8,128)S(1)} %get-tuple-element.45), channel_id=1, source_target_pairs={{0,4},{4,8},{8,12},{1,5},{5,9},{9,13},{2,6},{6,10},{10,14},{3,7},{... | collective-permute-start | bytes 393224 | tf_op jit(solution)/shard_map/ppermute | solution.py:27
  307.4 7.2 %collective-permute-start.17 = (f32[2,128,128]{2,1,0:T(8,128)S(1)}, f32[2,128,128]{2,1,0:T(8,128)S(1)}, u32[]{:S(2)}, u32[]{:S(2)}) collective-permute-start(f32[2,128,128]{2,1,0:T(8,128)S(1)} %get-tuple-element.46), channel_id=1, source_target_pairs={{4,0},{8,4},{12,8},{5,1},{9,5},{13,9},{6,2},{10,6},{14,10},{7,3},{... | collective-permute-start | bytes 393224 | tf_op jit(solution)/shard_map/ppermute | solution.py:27
  316.1 6.5 %collective-permute-start.19 = (f32[2,128,512]{2,1,0:T(8,128)}, f32[2,128,512]{2,1,0:T(8,128)}, u32[]{:S(2)}, u32[]{:S(2)}) collective-permute-start(f32[2,128,512]{2,1,0:T(8,128)} %pad_maximum_fusion.7), channel_id=1, source_target_pairs={{16,0},{17,1},{18,2},{19,3},{20,4},{21,5},{22,6},{23,7},{24,8},{25... | collective-permute-start | bytes 1572872 | tf_op jit(solution)/shard_map/ppermute | solution.py:27
  317.4 5.7 %collective-permute-start.18 = (f32[2,128,512]{2,1,0:T(8,128)}, f32[2,128,512]{2,1,0:T(8,128)}, u32[]{:S(2)}, u32[]{:S(2)}) collective-permute-start(f32[2,128,512]{2,1,0:T(8,128)} %pad_maximum_fusion.7), channel_id=1, source_target_pairs={{0,16},{1,17},{2,18},{3,19},{4,20},{5,21},{6,22},{7,23},{8,24},{9,... | collective-permute-start | bytes 1572872 | tf_op jit(solution)/shard_map/ppermute | solution.py:27
  333.5 43.5 %copy-start.8 = (f32[2,128,256]{2,1,0:T(8,128)S(1)}, f32[2,128,256]{2,1,0:T(8,128)}, u32[]{:S(2)}) copy-start(f32[2,128,256]{2,1,0:T(8,128)} %param.7) | copy-start | bytes 786436
  (13 other events, 45.2 us)
Sparse Core Ops, SparseCore 0:
  8.9 83.4 all-gather.5
  141.7 26.0 all-gather.7
  275.1 26.7 all-gather.9
